TPU v7x, 32 devices: a whole 2x2x4 slice. The times are simulated.
32 devices in a mesh: tok: 8 (over y, x, core), slot: 4 (over z).
Axes of the slice: x: 2, y: 2, z: 4, core: 2. Of those that a mesh axis runs over, the one named last changes fastest.
Arguments:
- tokens: bfloat16 [8192, 1024], P('tok'), may hold values from -16 to 16
- slot_params: bfloat16 [8192, 1024], P('slot'), may hold values from -0.5 to 0.5
- w_in: bfloat16 [16, 1024, 4096], P('slot', None, 'tok'), may hold values from -0.1875 to 0.1875
- w_out: bfloat16 [16, 4096, 1024], P('slot', 'tok'), may hold values from -0.09375 to 0.09375
Outputs:
- mixed: bfloat16 [8192, 1024], P(('tok', 'slot'))
All inputs are finite; a program needn't handle non-finite values.
Results may differ from a plain program's by a relative error of at most 0.01.
Values may be sent and summed in bfloat16 or wider, within the bound.
No kernel may reach another device: no remote copies, remote signals or barrier semaphores. Data moves between devices by JAX's collectives and lax.ppermute only.
A program may use at most 64 MiB of HBM per device.

v0:
```python
import jax
import jax.numpy as jnp
from jax import lax
from jax.sharding import PartitionSpec as P

P_SIZE = 8


def body(tokens, slot_params, w_in, w_out):
    experts_here = w_in.shape[0]
    in_flight = experts_here * P_SIZE
    logits = lax.dot_general(
        slot_params, tokens, (((1,), (1,)), ((), ())), preferred_element_type=jnp.float32
    )
    flight = logits[:in_flight]
    col_max = lax.pmax(jnp.max(flight, axis=1), "tok")
    dispatch_exp = jnp.exp(flight - col_max[:, None])
    dispatch_w = dispatch_exp.astype(jnp.bfloat16)
    numer = jnp.dot(dispatch_w, tokens, preferred_element_type=jnp.float32)
    numer, totals = lax.psum((numer, jnp.sum(dispatch_exp, axis=1)), "tok")
    slot_in = (
        (numer / totals[:, None]).astype(jnp.bfloat16).reshape(experts_here, P_SIZE, numer.shape[1])
    )
    pre_act = jnp.einsum("epd,edh->eph", slot_in, w_in, preferred_element_type=jnp.float32)
    hidden = jax.nn.gelu(pre_act).astype(jnp.bfloat16)
    partial_out = jnp.einsum("eph,ehd->epd", hidden, w_out, preferred_element_type=jnp.float32)
    partial_out = partial_out.reshape(in_flight, partial_out.shape[2])
    slot_out = lax.psum(partial_out, "tok").astype(jnp.bfloat16)
    row_max = lax.pmax(jnp.max(logits, axis=0), "slot")
    row_sum = lax.psum(jnp.sum(jnp.exp(logits - row_max[None, :]), axis=0), "slot")
    combine_w = (jnp.exp(flight - row_max[None, :]) / row_sum[None, :]).astype(jnp.bfloat16)
    token_weights = lax.all_to_all(combine_w, "slot", split_axis=1, concat_axis=0, tiled=True)
    all_outputs = lax.all_gather(slot_out, "slot", axis=0, tiled=True)
    mixed = lax.dot_general(
        token_weights, all_outputs, (((0,), (0,)), ((), ())), preferred_element_type=jnp.float32
    )
    return mixed.astype(jnp.bfloat16)


def solution(mesh):
    return jax.shard_map(
        body,
        mesh=mesh,
        in_specs=(P("tok", None), P("slot", None), P("slot", None, "tok"), P("slot", "tok", None)),
        out_specs=P(("tok", "slot"), None),
        check_vma=False,
    )
```

profile of v0, /device:TPU:0, one launch (start us, length us, event | category | flops | bytes accessed | tf_op | source)
XLA Modules:
  0.0 138.5 jit_solution(10838787701703055438)
XLA Ops:
  6.5 0.0 copy-start
  6.5 0.0 all-reduce.3.cloned.1.call-start
  6.5 1.6 %copy-done = bf16[1024,1024]{1,0:T(8,128)(2,1)S(1)} copy-done((bf16[1024,1024]{1,0:T(8,128)(2,1)S(1)}, bf16[1024,1024]{1,0:T(8,128)(2,1)}, u32[]{:S(2)}) %copy-start) | copy-done | bytes 2097176
  8.1 6.4 %fusion.27 = (f32[1024]{0:T(1024)S(1)}, f32[2048,1024]{1,0:T(8,128)S(1)}) fusion(bf16[2048,1024]{1,0:T(8,128)(2,1)} %param.5, bf16[1024,1024]{1,0:T(8,128)(2,1)S(1)} %copy-done), kind=kOutput, calls=%fused_computation.31 | convolution fusion | flops 4297063424 | bytes 14684160 | tf_op jit(solution)/shard_map/dot_general | solution.py:12
  14.5 0.0 copy-start.1
  14.5 3.2 %copy-done.1 = f32[2048,1024]{1,0:T(8,128)} copy-done((f32[2048,1024]{1,0:T(8,128)}, f32[2048,1024]{1,0:T(8,128)S(1)}, u32[]{:S(2)}) %copy-start.1) | copy-done | bytes 8388632
  17.7 0.1 slice_reduce_fusion
  17.8 15.2 %pmax.15 = f32[32]{0:T(128)S(1)} all-reduce(f32[32]{0:T(128)S(1)} %slice_reduce_fusion), channel_id=1, replica_groups=mesh['tok'=8,'slot'=4] {'tok'}, use_global_device_ids=true, to_apply=%region_5.0 | all-reduce | flops 32 | bytes 256 | tf_op jit(solution)/shard_map/pmax | solution.py:16
  33.0 2.1 %fusion.10 = f32[32,1024]{1,0:T(8,128)} fusion(bf16[1024,1024]{1,0:T(8,128)(2,1)S(1)} %copy-done, f32[2048,1024]{1,0:T(8,128)} %copy-done.1, f32[32]{0:T(128)S(1)} %pmax.15), kind=kOutput, calls=%fused_computation.18 | convolution fusion | flops 67174400 | bytes 2359424 | tf_op jit(solution)/shard_map/dot_general | solution.py:19
  35.1 0.0 all-reduce.3.cloned.1.call-update
  35.1 12.0 %pmax.14 = f32[1024]{0:T(1024)S(1)} all-reduce(f32[1024]{0:T(1024)S(1)} %get-tuple-element.7), channel_id=1, replica_groups=mesh['tok'=8,'slot'=4] {'slot'}, use_global_device_ids=true, to_apply=%region_1.0 | all-reduce | flops 1024 | bytes 8192 | tf_op jit(solution)/shard_map/pmax | solution.py:29
  47.1 4.6 %exponential_reduce_fusion = f32[1024]{0:T(1024)S(1)} fusion(f32[2048,1024]{1,0:T(8,128)} %copy-done.1, f32[1024]{0:T(1024)S(1)} %pmax.14), kind=kLoop, calls=%fused_computation | loop fusion | flops 4193280 | bytes 8396800 | tf_op jit(solution)/shard_map/reduce_sum | solution.py:30
  51.6 8.4 %psum.28 = f32[1024]{0:T(1024)S(1)} all-reduce(f32[1024]{0:T(1024)S(1)} %exponential_reduce_fusion), channel_id=1, replica_groups=mesh['tok'=8,'slot'=4] {'slot'}, use_global_device_ids=true, to_apply=%region_3.0 | all-reduce | flops 1024 | bytes 8192 | tf_op jit(solution)/shard_map/psum | solution.py:30
  60.0 1.1 fusion
  61.1 0.6 copy.8
  61.8 3.3 %all-to-all-start = ((bf16[32,4,256]{2,0,1:T(8,128)(2,1)}), bf16[32,4,256]{2,0,1:T(8,128)(2,1)S(1)}, u32[]{:S(2)}, u32[]{:S(2)}) async-start(bf16[32,4,256]{2,0,1:T(8,128)(2,1)} %bitcast.22), calls=%async_computation | async-start | bytes 131072 | tf_op jit(solution)/shard_map/all_to_all | solution.py:32
  65.0 11.9 %psum.30 = f32[32]{0:T(128)S(1)} all-reduce(f32[32]{0:T(128)S(1)} %get-tuple-element.5), channel_id=1, replica_groups=mesh['tok'=8,'slot'=4] {'tok'}, use_global_device_ids=true, to_apply=%region_8.0 | all-reduce | flops 32 | bytes 256 | tf_op jit(solution)/shard_map/psum | solution.py:20
  76.9 11.1 %all-reduce.3.cloned.1.call-done = f32[32,1024]{1,0:T(8,128)} async-done(((f32[32,1024]{1,0:T(8,128)}), f32[32,1024]{1,0:T(8,128)}) %all-reduce.3.cloned.1.call-update) | async-done | bytes 131088 | tf_op jit(solution)/shard_map/psum | solution.py:20
  88.1 4.7 %convolution_bitcast_fusion = f32[32,1024]{1,0:T(8,128)S(1)} fusion(bf16[4,512,1024]{2,1,0:T(8,128)(2,1)} %param.7, bf16[4,1024,512]{2,1,0:T(8,128)(2,1)} %param.6, f32[32,1024]{1,0:T(8,128)} %all-reduce.3.cloned.1.call-done, f32[32]{0:T(128)S(1)} %psum.30), kind=kOutput, calls=%fused_computation.2 | convolution fusion | flops 67321856 | bytes 8650880 | tf_op jit(solution)/shard_map/eph,ehd->epd/dot_general | solution.py:26
  92.8 23.4 %all-reduce.4 = bf16[32,1024]{1,0:T(8,128)(2,1)S(1)} all-reduce(f32[32,1024]{1,0:T(8,128)S(1)} %convolution_bitcast_fusion), channel_id=1, replica_groups=mesh['tok'=8,'slot'=4] {'tok'}, use_global_device_ids=true, to_apply=%region_9.0 | all-reduce | flops 32768 | bytes 196608 | tf_op jit(solution)/shard_map/psum | solution.py:28
  116.3 14.3 %all_gather.3 = bf16[128,1024]{1,0:T(8,128)(2,1)S(1)} all-gather(bf16[32,1024]{1,0:T(8,128)(2,1)S(1)} %all-reduce.4), channel_id=1, replica_groups=mesh['tok'=8,'slot'=4] {'slot'}, dimensions={0}, use_global_device_ids=true | all-gather | bytes 327680 | tf_op jit(solution)/shard_map/all_gather | solution.py:33
  130.6 0.0 all-to-all-done
  130.6 1.1 convolution_convert_fusion
Async XLA Ops:
  6.5 1.6 %copy-start = (bf16[1024,1024]{1,0:T(8,128)(2,1)S(1)}, bf16[1024,1024]{1,0:T(8,128)(2,1)}, u32[]{:S(2)}) copy-start(bf16[1024,1024]{1,0:T(8,128)(2,1)} %param.4) | copy-start | bytes 6291460
  6.5 81.5 %all-reduce.3.cloned.1.call-start = ((), (), s32[]{:S(2)}) async-start(), calls=%async_computation.1 | async-start | bytes 262144 | tf_op jit(solution)/shard_map/psum | solution.py:20
  14.5 3.2 %copy-start.1 = (f32[2048,1024]{1,0:T(8,128)}, f32[2048,1024]{1,0:T(8,128)S(1)}, u32[]{:S(2)}) copy-start(f32[2048,1024]{1,0:T(8,128)S(1)} %get-tuple-element.8) | copy-start | bytes 25165828
  61.8 68.8 %all-to-all-start = ((bf16[32,4,256]{2,0,1:T(8,128)(2,1)}), bf16[32,4,256]{2,0,1:T(8,128)(2,1)S(1)}, u32[]{:S(2)}, u32[]{:S(2)}) async-start(bf16[32,4,256]{2,0,1:T(8,128)(2,1)} %bitcast.22), calls=%async_computation | async-start | bytes 131072 | tf_op jit(solution)/shard_map/all_to_all | solution.py:32
Sparse Core Ops, SparseCore 0:
  35.2 52.7 all-reduce.2
where the time goes:
time: 139 us
  blocking collectives  85.1 us (61%)
  matrix products  14.3 us (10%)
  between operations  13.4 us (10%)
  waiting for transfers between devices  11.1 us (8%)
  other arithmetic  5.79 us (4%)
  local copies, waits for them, and re-layouts  5.43 us (4%)
  starting transfers between devices  3.29 us (2%)
    psum x1, blocking collectives, body(): slot_out = lax.psum(partial_out, 'tok').astype(jnp.bfloat16)  23.4 us
    pmax x1, blocking collectives, body(): col_max = lax.pmax(jnp.max(flight, axis=1), 'tok')  15.2 us
    all_gather x1, blocking collectives, body(): all_outputs = lax.all_gather(slot_out, 'slot', axis=0, tiled=True)  14.3 us
    pmax x1, blocking collectives, body(): row_max = lax.pmax(jnp.max(logits, axis=0), 'slot')  12 us
    psum x1, blocking collectives, body(): numer, totals = lax.psum((numer, jnp.sum(dispatch_exp, axis=1)), 'tok')  11.9 us
    psum x1, waiting for transfers between devices, body(): numer, totals = lax.psum((numer, jnp.sum(dispatch_exp, axis=1)), 'tok')  11.1 us
    psum x1, blocking collectives, body(): lax.psum(jnp.sum(jnp.exp(logits - row_max[None, :]), axis=0), 'slot')  8.37 us
    dot_general x1, matrix products, body(): lax.dot_general(slot_params, tokens, (((1,), (1,)), ((), ())), preferred_...  6.38 us
  transfers between devices with their start and end apart: 2, of which 1 were waited for; matrix products, arithmetic and copies ran while one was open for 8% of the time, Pallas kernels for 0%

commit v1 on v0

v1 whole, which is shorter than its diff:
```python
import functools

import jax
import jax.numpy as jnp
from jax import lax
from jax.experimental import pallas as pl
from jax.experimental.pallas import tpu as pltpu
from jax.sharding import PartitionSpec as P

P_SIZE = 8
LANES = 128
BF = jnp.bfloat16
F32 = jnp.float32
VMEM = pl.BlockSpec(memory_space=pltpu.VMEM)
SMEM = pl.BlockSpec(memory_space=pltpu.SMEM)


def sds(shape, dtype):
    return jax.ShapeDtypeStruct(shape, dtype)


def call(kernel, outs, n_in, name, flops=0, vmem=None, scalars=0, **kw):
    return pl.pallas_call(
        kernel,
        out_shape=outs,
        in_specs=kw.pop("in_specs", [SMEM] * scalars + [VMEM] * n_in),
        out_specs=jax.tree.map(lambda _: VMEM, outs),
        name=name,
        compiler_params=pltpu.CompilerParams(vmem_limit_bytes=vmem),
        cost_estimate=pl.CostEstimate(flops=flops, bytes_accessed=0, transcendentals=0),
        **kw,
    )


def lane_pack(rows, *columns):
    lane = lax.broadcasted_iota(jnp.int32, (rows, LANES), 1)
    out = jnp.zeros((rows, LANES), F32)
    for k, column in enumerate(columns):
        out = jnp.where(lane == k, column, out)
    return out


def write_state(num, top, tot, num_ref, st_ref, msg_ref):
    rows, d = num.shape
    num_ref[...] = num
    st_ref[...] = lane_pack(rows, top, tot)
    hi = tot.astype(BF).astype(F32)
    lo = (tot - hi).astype(BF).astype(F32)
    msg_ref[:, :d] = num.astype(BF)
    msg_ref[:, d:] = lane_pack(rows, top, hi, lo).astype(BF)


def dispatch_kernel(sp_ref, tok_ref, flight_ref, num_ref, st_ref, msg_ref):
    tok = tok_ref[...]
    flight = lax.dot_general(sp_ref[...], tok, (((1,), (1,)), ((), ())), preferred_element_type=F32)
    flight_ref[...] = flight
    top = jnp.max(flight, axis=1, keepdims=True).astype(BF).astype(F32)
    e = jnp.exp(flight - top)
    tot = jnp.sum(e, axis=1, keepdims=True)
    num = jnp.dot(e.astype(BF), tok, preferred_element_type=F32)
    write_state(num, top, tot, num_ref, st_ref, msg_ref)


def merge(num_ref, st_ref, recv_ref):
    d = num_ref.shape[1]
    top, tot = st_ref[:, 0:1], st_ref[:, 1:2]
    rs = recv_ref[:, d:].astype(F32)
    rtop, rtot = rs[:, 0:1], rs[:, 1:2] + rs[:, 2:3]
    new = jnp.maximum(top, rtop)
    a, b = jnp.exp(top - new), jnp.exp(rtop - new)
    num = num_ref[...] * a + recv_ref[:, :d].astype(F32) * b
    return num, new, tot * a + rtot * b


def merge_kernel(num_ref, st_ref, recv_ref, num_out, st_out, msg_out):
    write_state(*merge(num_ref, st_ref, recv_ref), num_out, st_out, msg_out)


def merge_last_kernel(num_ref, st_ref, recv_ref, out_ref):
    num, _, tot = merge(num_ref, st_ref, recv_ref)
    out_ref[...] = (num / tot).astype(BF)


def mlp_kernel(north_ref, own_ref, recv_ref, win_ref, wout_ref, out_ref, msg_ref):
    x = jnp.where(north_ref[0] == 1, own_ref[...].astype(F32), recv_ref[...].astype(F32))
    experts = win_ref.shape[0]
    for e in range(experts):
        rows = slice(e * P_SIZE, (e + 1) * P_SIZE)
        pre = jnp.dot(x[rows].astype(BF), win_ref[e], preferred_element_type=F32)
        hidden = jax.nn.gelu(pre).astype(BF)
        out_ref[rows, :] = jnp.dot(hidden, wout_ref[e], preferred_element_type=F32)
    msg_ref[...] = out_ref[...].astype(BF)


def stats_kernel(first, step, sp_ref, tok_ref, m_ref, l_ref, mo_ref, lo_ref):
    rows, n = sp_ref.shape[0], tok_ref.shape[0]
    if first:
        m, l = jnp.full((8, n), -jnp.inf, F32), jnp.zeros((8, n), F32)
    else:
        m, l = m_ref[...], l_ref[...]
    tok = tok_ref[...]
    for r in range(0, rows, step):
        x = lax.dot_general(
            sp_ref[r : r + step, :], tok, (((1,), (1,)), ((), ())), preferred_element_type=F32
        ).reshape(step // 8, 8, n)
        new = jnp.maximum(m, jnp.max(x, axis=0))
        l = l * jnp.exp(m - new) + jnp.sum(jnp.exp(x - new[None]), axis=0)
        m = new
    mo_ref[...] = m
    lo_ref[...] = l


def pack_kernel(flight_ref, m_ref, l_ref, out_ref):
    rows = flight_ref.shape[0]
    m, l = m_ref[...], l_ref[...]
    top = jnp.max(m, axis=0, keepdims=True)
    tot = jnp.sum(l * jnp.exp(m - top), axis=0, keepdims=True)
    out_ref[:rows, :] = flight_ref[...]
    sub = lax.broadcasted_iota(jnp.int32, m.shape, 0)
    out_ref[rows:, :] = jnp.where(sub == 0, top, jnp.where(sub == 1, tot, 0.0))


def weights_kernel(*refs):
    parts, out_ref = refs[:-1], refs[-1]
    rows = parts[0].shape[0] - 8
    tops = [p[rows : rows + 1, :] for p in parts]
    top = functools.reduce(jnp.maximum, tops)
    tot = sum(p[rows + 1 : rows + 2, :] * jnp.exp(t - top) for p, t in zip(parts, tops))
    w = jnp.concatenate([jnp.exp(p[:rows, :] - top) / tot for p in parts], axis=0)
    out_ref[...] = w.T.astype(BF)


def combine_kernel(pieces, north_ref, w_ref, *refs):
    own, recv, out_ref = refs[:pieces], refs[pieces : 2 * pieces], refs[2 * pieces]
    scratch = refs[2 * pieces + 1]
    at = 0
    for a, b in zip(own, recv):
        n = a.shape[0]
        scratch[at : at + n, :] = jnp.where(north_ref[0] == 1, a[...], b[...])
        at += n
    out_ref[...] = jnp.dot(w_ref[...], scratch[...], preferred_element_type=F32).astype(BF)


def body(n_tok, n_slot, tokens, slot_params, w_in, w_out):
    n, d = tokens.shape
    experts, _, h = w_in.shape
    rows = experts * P_SIZE
    me_slot = lax.axis_index("slot")
    odd = lax.rem(lax.axis_index("tok"), 2)
    north = odd.astype(jnp.int32).reshape(1)

    def up(x):
        return lax.ppermute(x, "tok", [(i, i + 1) for i in range(0, n_tok, 2)])

    def down(x):
        return lax.ppermute(x, "tok", [(i + 1, i) for i in range(0, n_tok, 2)])

    def swap_tok(x, bit):
        return lax.ppermute(x, "tok", [(i, i ^ bit) for i in range(1, n_tok, 2)])

    def swap_slot(x, bit):
        pairs = [(i * n_slot + j, i * n_slot + (j ^ bit)) for i in range(1, n_tok, 2) for j in range(n_slot)]
        return lax.ppermute(x, ("tok", "slot"), pairs)

    tok_bits = [1 << b for b in range(1, n_tok.bit_length() - 1)]
    slot_bits = [1 << b for b in range(n_slot.bit_length() - 1)]

    state = [sds((rows, d), F32), sds((rows, LANES), F32), sds((rows, d + LANES), BF)]
    flight, num, st, msg = call(
        dispatch_kernel, [sds((rows, n), F32)] + state, 2, "dispatch", flops=4 * rows * n * d, vmem=8 << 20
    )(slot_params[:rows], tokens)
    recv = up(msg)
    for bit in tok_bits:
        num, st, msg = call(merge_kernel, state, 3, "merge", vmem=2 << 20)(num, st, recv)
        recv = swap_tok(msg, bit)
    slot_in = call(merge_last_kernel, sds((rows, d), BF), 3, "merge_last", vmem=2 << 20)(num, st, recv)
    recv = down(slot_in)

    slots = slot_params.shape[0]
    chunk = min(512, slots)
    m = jnp.zeros((8, n), F32)
    l = m
    for c in range(0, slots, chunk):
        m, l = call(
            functools.partial(stats_kernel, c == 0, min(256, chunk)),
            [sds((8, n), F32)] * 2,
            4,
            "stats",
            flops=2 * chunk * n * d,
            vmem=12 << 20,
            grid=(1,),
            in_specs=[
                pl.BlockSpec((chunk, d), lambda i, c=c: (c // chunk, 0)),
                VMEM,
                VMEM,
                VMEM,
            ],
        )(slot_params, tokens, m, l)
    pack = call(pack_kernel, sds((rows + 8, n), F32), 3, "pack", vmem=2 << 20)(flight, m, l)
    share = n // n_slot
    parts = []
    for k in range(n_slot):
        part = lax.dynamic_slice_in_dim(pack, (me_slot ^ k) * share, share, axis=1)
        if k:
            part = lax.ppermute(part, "slot", [(j, j ^ k) for j in range(n_slot)])
        parts.append(part)
    weights = call(weights_kernel, sds((share, n_slot * rows), BF), n_slot, "weights", vmem=4 << 20)(*parts)

    out, msg = call(
        mlp_kernel,
        [sds((rows, d), F32), sds((rows, d), BF)],
        4,
        "mlp",
        flops=4 * rows * d * h,
        vmem=12 << 20,
        scalars=1,
    )(north, slot_in, recv, w_in, w_out)
    out = out + up(msg).astype(F32)
    for bit in tok_bits:
        out = out + swap_tok(out.astype(BF), bit).astype(F32)
    own = [out.astype(BF)]
    for bit in slot_bits:
        have = own[0] if len(own) == 1 else jnp.concatenate(own, axis=0)
        own.append(swap_slot(have, bit))
    below = [down(x) for x in own]
    return pl.pallas_call(
        functools.partial(combine_kernel, len(own)),
        out_shape=sds((share, d), BF),
        in_specs=[SMEM] + [VMEM] * (1 + 2 * len(own)),
        out_specs=VMEM,
        scratch_shapes=[pltpu.VMEM((n_slot * rows, d), BF)],
        name="combine",
        compiler_params=pltpu.CompilerParams(vmem_limit_bytes=8 << 20),
    )(north, weights, *own, *below)


def solution(mesh):
    sizes = dict(mesh.shape)
    return jax.shard_map(
        functools.partial(body, sizes["tok"], sizes["slot"]),
        mesh=mesh,
        in_specs=(P("tok", None), P("slot", None), P("slot", None, "tok"), P("slot", "tok", None)),
        out_specs=P(("tok", "slot"), None),
        check_vma=False,
    )
```

time: 139 us -> 66.2 us (0.48)
  the two profiles are of different devices: /device:TPU:0 before, /device:TPU:1 now
where the time goes in v1:
time: 66.2 us; the launch traced here: 65.6 us
  starting transfers between devices  33.4 us (50%)
  waiting for transfers between devices  12.1 us (18%)
  Pallas kernels  10.8 us (16%)
  local copies, waits for them, and re-layouts  9.03 us (14%)
    ppermute x4, starting transfers between devices, swap_tok(): return lax.ppermute(x, 'tok', [(i, i ^ bit) for i in range(1, n_tok, 2)])  14 us
    unnamed x12, local copies, waits for them, and re-layouts  8.16 us
    ppermute x2, starting transfers between devices, swap_slot(): return lax.ppermute(x, ('tok', 'slot'), pairs)  7.8 us
    pallas_call x4, Pallas kernels, body(): call(functools.partial(stats_kernel, c == 0, min(256, chunk)), [sds((8, n...  6.19 us
    ppermute x4, waiting for transfers between devices, swap_tok(): return lax.ppermute(x, 'tok', [(i, i ^ bit) for i in range(1, n_tok, 2)])  5.17 us
    ppermute x4, starting transfers between devices, down(): return lax.ppermute(x, 'tok', [(i + 1, i) for i in range(0, n_tok, 2)])  5.16 us
    ppermute x2, waiting for transfers between devices, up(): return lax.ppermute(x, 'tok', [(i, i + 1) for i in range(0, n_tok, 2)])  3.71 us
    ppermute x3, starting transfers between devices, body(): part = lax.ppermute(part, 'slot', [(j, j ^ k) for j in range(n_slot)])  3.68 us
  transfers between devices with their start and end apart: 15, of which 9 were waited for; matrix products, arithmetic and copies ran while one was open for 0% of the time, Pallas kernels for 10%

profile of v1, /device:TPU:1, one launch (start us, length us, event | category | flops | bytes accessed | tf_op | source)
XLA Modules:
  0.0 65.6 jit_solution(17932632890657906407)
XLA Ops:
  0.0 0.8 %slice.3.sp_ref = bf16[32,1024]{1,0:T(8,128)(2,1)S(1)} slice(bf16[2048,1024]{1,0:T(8,128)(2,1)} %sp_ref.7), slice={[0:32], [0:1024]} | slice | bytes 131072 | tf_op jit(solution)/shard_map/slice | solution.py:171
  0.8 0.0 copy-start.2
  0.8 1.6 %copy-done.2 = bf16[1024,1024]{1,0:T(8,128)(2,1)S(1)} copy-done((bf16[1024,1024]{1,0:T(8,128)(2,1)S(1)}, bf16[1024,1024]{1,0:T(8,128)(2,1)}, u32[]{:S(2)}) %copy-start.2) | copy-done | bytes 2097176
  2.4 1.2 %dispatch.1 = (f32[32,1024]{1,0:T(8,128)S(1)}, f32[32,1024]{1,0:T(8,128)S(1)}, f32[32,128]{1,0:T(8,128)S(1)}, bf16[32,1152]{1,0:T(8,128)(2,1)S(1)}) custom-call(bf16[32,1024]{1,0:T(8,128)(2,1)S(1)} %slice.3.sp_ref, bf16[1024,1024]{1,0:T(8,128)(2,1)S(1)} %copy-done.2), custom_call_target="tpu_custom_call" | custom-call | flops 134217728 | tf_op jit(solution)/shard_map/dispatch/pallas_call | solution.py:169
  3.7 1.3 %collective-permute-start.3 = (bf16[32,1152]{1,0:T(8,128)(2,1)S(1)}, bf16[32,1152]{1,0:T(8,128)(2,1)S(1)}, u32[]{:S(2)}, u32[]{:S(2)}) collective-permute-start(bf16[32,1152]{1,0:T(8,128)(2,1)S(1)} %get-tuple-element.36), channel_id=1, source_target_pairs={{0,4},{8,12},{16,20},{24,28},{1,5},{9,13},{17,21},{25,29},{2,6},{1... | collective-permute-start | bytes 221192 | tf_op jit(solution)/shard_map/ppermute | solution.py:153
  5.0 1.9 %collective-permute-done.3.recv_ref = bf16[32,1152]{1,0:T(8,128)(2,1)S(1)} collective-permute-done((bf16[32,1152]{1,0:T(8,128)(2,1)S(1)}, bf16[32,1152]{1,0:T(8,128)(2,1)S(1)}, u32[]{:S(2)}, u32[]{:S(2)}) %collective-permute-start.3) | collective-permute-done | bytes 73760 | tf_op jit(solution)/shard_map/ppermute | solution.py:153
  6.8 0.2 merge.2
  7.0 3.9 %collective-permute-start.4 = (bf16[32,1152]{1,0:T(8,128)(2,1)S(1)}, bf16[32,1152]{1,0:T(8,128)(2,1)S(1)}, u32[]{:S(2)}, u32[]{:S(2)}) collective-permute-start(bf16[32,1152]{1,0:T(8,128)(2,1)S(1)} %get-tuple-element.39), channel_id=1, source_target_pairs={{4,12},{12,4},{20,28},{28,20},{5,13},{13,5},{21,29},{29,21},{6,14}... | collective-permute-start | bytes 221192 | tf_op jit(solution)/shard_map/ppermute | solution.py:159
  11.0 1.7 %collective-permute-done.4.recv_ref = bf16[32,1152]{1,0:T(8,128)(2,1)S(1)} collective-permute-done((bf16[32,1152]{1,0:T(8,128)(2,1)S(1)}, bf16[32,1152]{1,0:T(8,128)(2,1)S(1)}, u32[]{:S(2)}, u32[]{:S(2)}) %collective-permute-start.4) | collective-permute-done | bytes 73760 | tf_op jit(solution)/shard_map/ppermute | solution.py:159
  12.7 0.2 merge.3
  12.9 3.4 %collective-permute-start.5 = (bf16[32,1152]{1,0:T(8,128)(2,1)S(1)}, bf16[32,1152]{1,0:T(8,128)(2,1)S(1)}, u32[]{:S(2)}, u32[]{:S(2)}) collective-permute-start(bf16[32,1152]{1,0:T(8,128)(2,1)S(1)} %get-tuple-element.42), channel_id=1, source_target_pairs={{4,20},{12,28},{20,4},{28,12},{5,21},{13,29},{21,5},{29,13},{6,22}... | collective-permute-start | bytes 221192 | tf_op jit(solution)/shard_map/ppermute | solution.py:159
  16.2 1.7 %collective-permute-done.5.recv_ref = bf16[32,1152]{1,0:T(8,128)(2,1)S(1)} collective-permute-done((bf16[32,1152]{1,0:T(8,128)(2,1)S(1)}, bf16[32,1152]{1,0:T(8,128)(2,1)S(1)}, u32[]{:S(2)}, u32[]{:S(2)}) %collective-permute-start.5) | collective-permute-done | bytes 73760 | tf_op jit(solution)/shard_map/ppermute | solution.py:159
  18.0 0.2 merge_last.1.own_ref
  18.2 1.3 %collective-permute-start.6 = (bf16[32,1024]{1,0:T(8,128)(2,1)S(1)}, bf16[32,1024]{1,0:T(8,128)(2,1)S(1)}, u32[]{:S(2)}, u32[]{:S(2)}) collective-permute-start(bf16[32,1024]{1,0:T(8,128)(2,1)S(1)} %merge_last.1.own_ref), channel_id=1, source_target_pairs={{4,0},{12,8},{20,16},{28,24},{5,1},{13,9},{21,17},{29,25},{6,2},{1... | collective-permute-start | bytes 196616 | tf_op jit(solution)/shard_map/ppermute | solution.py:156
  19.5 0.9 %collective-permute-done.6.recv_ref = bf16[32,1024]{1,0:T(8,128)(2,1)S(1)} collective-permute-done((bf16[32,1024]{1,0:T(8,128)(2,1)S(1)}, bf16[32,1024]{1,0:T(8,128)(2,1)S(1)}, u32[]{:S(2)}, u32[]{:S(2)}) %collective-permute-start.6) | collective-permute-done | bytes 65568 | tf_op jit(solution)/shard_map/ppermute | solution.py:156
  20.3 0.0 copy-start.4
  20.3 2.2 %copy-done.4 = bf16[4,1024,512]{2,1,0:T(8,128)(2,1)S(1)} copy-done((bf16[4,1024,512]{2,1,0:T(8,128)(2,1)S(1)}, bf16[4,1024,512]{2,1,0:T(8,128)(2,1)}, u32[]{:S(2)}) %copy-start.4) | copy-done | bytes 4194328
  22.5 0.0 copy-start.5
  22.5 2.2 %copy-done.5 = bf16[4,512,1024]{2,1,0:T(8,128)(2,1)S(1)} copy-done((bf16[4,512,1024]{2,1,0:T(8,128)(2,1)S(1)}, bf16[4,512,1024]{2,1,0:T(8,128)(2,1)}, u32[]{:S(2)}) %copy-start.5) | copy-done | bytes 4194328
  24.7 0.0 copy-start
  24.7 0.0 copy-start.3
  24.7 1.6 %mlp.1 = (f32[32,1024]{1,0:T(8,128)S(1)}, bf16[32,1024]{1,0:T(8,128)(2,1)S(1)}) custom-call(s32[1]{0:T(128)} %bitcast.north_ref, bf16[32,1024]{1,0:T(8,128)(2,1)S(1)} %merge_last.1.own_ref, bf16[32,1024]{1,0:T(8,128)(2,1)S(1)} %collective-permute-done.6.recv_ref, bf16[4,1024,512]{2,1,0:T(8,128)(2,1)S(1)} %copy-done.4, bf16[4,512,1024]{2,1,0:T(8,128)(2,1)S(1)} %copy-done.5), custom_call_target="tpu_custom_call" | custom-call | flops 67108864 | tf_op jit(solution)/shard_map/mlp/pallas_call | solution.py:209
  26.3 1.4 %collective-permute-start.7 = (bf16[32,1024]{1,0:T(8,128)(2,1)S(1)}, bf16[32,1024]{1,0:T(8,128)(2,1)S(1)}, u32[]{:S(2)}, u32[]{:S(2)}) collective-permute-start(bf16[32,1024]{1,0:T(8,128)(2,1)S(1)} %get-tuple-element.44), channel_id=1, source_target_pairs={{0,4},{8,12},{16,20},{24,28},{1,5},{9,13},{17,21},{25,29},{2,6},{1... | collective-permute-start | bytes 196616 | tf_op jit(solution)/shard_map/ppermute | solution.py:153
  27.7 1.8 %collective-permute-done.7 = bf16[32,1024]{1,0:T(8,128)(2,1)S(1)} collective-permute-done((bf16[32,1024]{1,0:T(8,128)(2,1)S(1)}, bf16[32,1024]{1,0:T(8,128)(2,1)S(1)}, u32[]{:S(2)}, u32[]{:S(2)}) %collective-permute-start.7) | collective-permute-done | bytes 65568 | tf_op jit(solution)/shard_map/ppermute | solution.py:153
  29.6 3.3 %collective-permute-start.8 = (bf16[32,1024]{1,0:T(8,128)(2,1)S(1)}, bf16[32,1024]{1,0:T(8,128)(2,1)S(1)}, u32[]{:S(2)}, u32[]{:S(2)}) collective-permute-start(bf16[32,1024]{1,0:T(8,128)(2,1)S(1)} %fusion), channel_id=1, source_target_pairs={{4,12},{12,4},{20,28},{28,20},{5,13},{13,5},{21,29},{29,21},{6,14}... | collective-permute-start | bytes 196616 | tf_op jit(solution)/shard_map/ppermute | solution.py:159
  32.9 1.7 %collective-permute-done.8 = bf16[32,1024]{1,0:T(8,128)(2,1)S(1)} collective-permute-done((bf16[32,1024]{1,0:T(8,128)(2,1)S(1)}, bf16[32,1024]{1,0:T(8,128)(2,1)S(1)}, u32[]{:S(2)}, u32[]{:S(2)}) %collective-permute-start.8) | collective-permute-done | bytes 65568 | tf_op jit(solution)/shard_map/ppermute | solution.py:159
  34.6 3.4 %collective-permute-start.9 = (bf16[32,1024]{1,0:T(8,128)(2,1)S(1)}, bf16[32,1024]{1,0:T(8,128)(2,1)S(1)}, u32[]{:S(2)}, u32[]{:S(2)}) collective-permute-start(bf16[32,1024]{1,0:T(8,128)(2,1)S(1)} %fusion.1), channel_id=1, source_target_pairs={{4,20},{12,28},{20,4},{28,12},{5,21},{13,29},{21,5},{29,13},{6,22}... | collective-permute-start | bytes 196616 | tf_op jit(solution)/shard_map/ppermute | solution.py:159
  38.0 0.0 copy-done
  38.0 0.0 copy-done.3
  38.0 1.6 %stats.4 = (f32[8,1024]{1,0:T(8,128)S(1)}, f32[8,1024]{1,0:T(8,128)S(1)}) custom-call(bf16[2048,1024]{1,0:T(8,128)(2,1)S(1)} %copy-done, bf16[1024,1024]{1,0:T(8,128)(2,1)S(1)} %copy-done.3, f32[8,1024]{1,0:T(8,128)S(1)} %broadcast_in_dim.3.m_ref.l_ref, f32[8,1024]{1,0:T(8,128)S(1)} %broadcast_in_dim.3.m_ref.l_ref), custom_call_target="tpu_custom_call" | custom-call | flops 1073741824 | tf_op jit(solution)/shard_map/stats/pallas_call | solution.py:184
  39.6 0.1 collective-permute-done.9
  39.7 3.4 %collective-permute-start.10 = (bf16[32,1024]{1,0:T(8,128)(2,1)S(1)}, bf16[32,1024]{1,0:T(8,128)(2,1)S(1)}, u32[]{:S(2)}, u32[]{:S(2)}) collective-permute-start(bf16[32,1024]{1,0:T(8,128)(2,1)S(1)} %add_convert_fusion.refs_0_), channel_id=1, source_target_pairs={{4,5},{5,4},{6,7},{7,6},{12,13},{13,12},{14,15},{15,14},{20,21},{2... | collective-permute-start | bytes 196616 | tf_op jit(solution)/shard_map/ppermute | solution.py:163
  43.1 1.6 %stats.5 = (f32[8,1024]{1,0:T(8,128)S(1)}, f32[8,1024]{1,0:T(8,128)S(1)}) custom-call(bf16[2048,1024]{1,0:T(8,128)(2,1)S(1)} %copy-done, bf16[1024,1024]{1,0:T(8,128)(2,1)S(1)} %copy-done.3, f32[8,1024]{1,0:T(8,128)S(1)} %get-tuple-element.26.m_ref, f32[8,1024]{1,0:T(8,128)S(1)} %get-tuple-element.27.l_ref), custom_call_target="tpu_custom_call" | custom-call | flops 1073741824 | tf_op jit(solution)/shard_map/stats/pallas_call | solution.py:184
  44.7 0.1 collective-permute-done.10.refs_1_
  44.8 4.4 %collective-permute-start.11 = (bf16[64,1024]{1,0:T(8,128)(2,1)S(1)}, bf16[64,1024]{1,0:T(8,128)(2,1)S(1)}, u32[]{:S(2)}, u32[]{:S(2)}) collective-permute-start(bf16[64,1024]{1,0:T(8,128)(2,1)S(1)} %pad_maximum_fusion), channel_id=1, source_target_pairs={{4,6},{5,7},{6,4},{7,5},{12,14},{13,15},{14,12},{15,13},{20,22},{2... | collective-permute-start | bytes 393224 | tf_op jit(solution)/shard_map/ppermute | solution.py:163
  49.2 1.6 %stats.6 = (f32[8,1024]{1,0:T(8,128)S(1)}, f32[8,1024]{1,0:T(8,128)S(1)}) custom-call(bf16[2048,1024]{1,0:T(8,128)(2,1)S(1)} %copy-done, bf16[1024,1024]{1,0:T(8,128)(2,1)S(1)} %copy-done.3, f32[8,1024]{1,0:T(8,128)S(1)} %get-tuple-element.28.m_ref, f32[8,1024]{1,0:T(8,128)S(1)} %get-tuple-element.29.l_ref), custom_call_target="tpu_custom_call" | custom-call | flops 1073741824 | tf_op jit(solution)/shard_map/stats/pallas_call | solution.py:184
  50.7 0.0 copy-start.1
  50.7 2.2 %copy-done.1 = bf16[2048,1024]{1,0:T(8,128)(2,1)S(1)} copy-done((bf16[2048,1024]{1,0:T(8,128)(2,1)S(1)}, bf16[2048,1024]{1,0:T(8,128)(2,1)}, u32[]{:S(2)}) %copy-start.1) | copy-done | bytes 4194328
  52.9 1.5 %stats.7 = (f32[8,1024]{1,0:T(8,128)S(1)}, f32[8,1024]{1,0:T(8,128)S(1)}) custom-call(bf16[2048,1024]{1,0:T(8,128)(2,1)S(1)} %copy-done.1, bf16[1024,1024]{1,0:T(8,128)(2,1)S(1)} %copy-done.3, f32[8,1024]{1,0:T(8,128)S(1)} %get-tuple-element.30.m_ref, f32[8,1024]{1,0:T(8,128)S(1)} %get-tuple-element.31.l_ref), custom_call_target="tpu_custom_call" | custom-call | flops 1073741824 | tf_op jit(solution)/shard_map/stats/pallas_call | solution.py:184
  54.5 0.0 collective-permute-done.11.refs_2_
  54.5 1.3 %collective-permute-start.14 = (bf16[64,1024]{1,0:T(8,128)(2,1)S(1)}, bf16[64,1024]{1,0:T(8,128)(2,1)S(1)}, u32[]{:S(2)}, u32[]{:S(2)}) collective-permute-start(bf16[64,1024]{1,0:T(8,128)(2,1)S(1)} %collective-permute-done.11.refs_2_), channel_id=1, source_target_pairs={{4,0},{12,8},{20,16},{28,24},{5,1},{13,9},{21,17},{29,25},{6,2},{1... | collective-permute-start | bytes 393224 | tf_op jit(solution)/shard_map/ppermute | solution.py:156
  55.8 2.1 %collective-permute-start.2 = (f32[40,256]{1,0:T(8,128)S(1)}, f32[40,256]{1,0:T(8,128)S(1)}, u32[]{:S(2)}, u32[]{:S(2)}) collective-permute-start(f32[40,256]{1,0:T(8,128)S(1)} %get-tuple-element.45), channel_id=1, source_target_pairs={{0,3},{1,2},{2,1},{3,0},{4,7},{5,6},{6,5},{7,4},{8,11},{9,10},{10,... | collective-permute-start | bytes 122888 | tf_op jit(solution)/shard_map/ppermute | solution.py:205
  58.0 1.3 %collective-permute-start.12 = (bf16[32,1024]{1,0:T(8,128)(2,1)S(1)}, bf16[32,1024]{1,0:T(8,128)(2,1)S(1)}, u32[]{:S(2)}, u32[]{:S(2)}) collective-permute-start(bf16[32,1024]{1,0:T(8,128)(2,1)S(1)} %add_convert_fusion.refs_0_), channel_id=1, source_target_pairs={{4,0},{12,8},{20,16},{28,24},{5,1},{13,9},{21,17},{29,25},{6,2},{1... | collective-permute-start | bytes 196616 | tf_op jit(solution)/shard_map/ppermute | solution.py:156
  59.3 1.3 %collective-permute-start.13 = (bf16[32,1024]{1,0:T(8,128)(2,1)S(1)}, bf16[32,1024]{1,0:T(8,128)(2,1)S(1)}, u32[]{:S(2)}, u32[]{:S(2)}) collective-permute-start(bf16[32,1024]{1,0:T(8,128)(2,1)S(1)} %collective-permute-done.10.refs_1_), channel_id=1, source_target_pairs={{4,0},{12,8},{20,16},{28,24},{5,1},{13,9},{21,17},{29,25},{6,2},{1... | collective-permute-start | bytes 196616 | tf_op jit(solution)/shard_map/ppermute | solution.py:156
  60.6 0.5 collective-permute-start.1
  61.1 0.0 collective-permute-done.2.refs_3_
  61.1 1.1 %collective-permute-start = (f32[40,256]{1,0:T(8,128)S(1)}, f32[40,256]{1,0:T(8,128)S(1)}, u32[]{:S(2)}, u32[]{:S(2)}) collective-permute-start(f32[40,256]{1,0:T(8,128)S(1)} %get-tuple-element.47), channel_id=1, source_target_pairs={{0,1},{1,0},{2,3},{3,2},{4,5},{5,4},{6,7},{7,6},{8,9},{9,8},{10,11... | collective-permute-start | bytes 122888 | tf_op jit(solution)/shard_map/ppermute | solution.py:205
  62.1 2.3 %collective-permute-done.1.refs_2_ = f32[40,256]{1,0:T(8,128)S(1)} collective-permute-done((f32[40,256]{1,0:T(8,128)S(1)}, f32[40,256]{1,0:T(8,128)S(1)}, u32[]{:S(2)}, u32[]{:S(2)}) %collective-permute-start.1) | collective-permute-done | bytes 40992 | tf_op jit(solution)/shard_map/ppermute | solution.py:205
  64.4 0.0 collective-permute-done.refs_1_
  64.4 0.1 weights.1.w_ref
  64.5 0.0 collective-permute-done.12.refs_3_
  64.5 0.0 collective-permute-done.13.refs_4_
  64.5 0.0 collective-permute-done.14.refs_5_
  64.5 1.1 %combine.1 = bf16[256,1024]{1,0:T(8,128)(2,1)} custom-call(s32[1]{0:T(128)} %bitcast.north_ref, bf16[256,128]{1,0:T(8,128)(2,1)S(1)} %weights.1.w_ref, bf16[32,1024]{1,0:T(8,128)(2,1)S(1)} %add_convert_fusion.refs_0_, bf16[32,1024]{1,0:T(8,128)(2,1)S(1)} %collective-permute-done.10.refs_1_, bf16[64,1024]{1,0:T(8,128)(2,1)S(1)} %collective-permute-done.11.refs_2_, ...), custom_call_target="tpu_custom_call" | custom-call | tf_op jit(solution)/shard_map/combine/pallas_call | solution.py:226
  (7 shorter events, 0.2 us)
Async XLA Ops:
  0.8 1.6 %copy-start.2 = (bf16[1024,1024]{1,0:T(8,128)(2,1)S(1)}, bf16[1024,1024]{1,0:T(8,128)(2,1)}, u32[]{:S(2)}) copy-start(bf16[1024,1024]{1,0:T(8,128)(2,1)} %tok_ref.9) | copy-start | bytes 6291460
  3.7 3.2 %collective-permute-start.3 = (bf16[32,1152]{1,0:T(8,128)(2,1)S(1)}, bf16[32,1152]{1,0:T(8,128)(2,1)S(1)}, u32[]{:S(2)}, u32[]{:S(2)}) collective-permute-start(bf16[32,1152]{1,0:T(8,128)(2,1)S(1)} %get-tuple-element.36), channel_id=1, source_target_pairs={{0,4},{8,12},{16,20},{24,28},{1,5},{9,13},{17,21},{25,29},{2,6},{1... | collective-permute-start | bytes 221192 | tf_op jit(solution)/shard_map/ppermute | solution.py:153
  7.0 5.7 %collective-permute-start.4 = (bf16[32,1152]{1,0:T(8,128)(2,1)S(1)}, bf16[32,1152]{1,0:T(8,128)(2,1)S(1)}, u32[]{:S(2)}, u32[]{:S(2)}) collective-permute-start(bf16[32,1152]{1,0:T(8,128)(2,1)S(1)} %get-tuple-element.39), channel_id=1, source_target_pairs={{4,12},{12,4},{20,28},{28,20},{5,13},{13,5},{21,29},{29,21},{6,14}... | collective-permute-start | bytes 221192 | tf_op jit(solution)/shard_map/ppermute | solution.py:159
  12.9 5.1 %collective-permute-start.5 = (bf16[32,1152]{1,0:T(8,128)(2,1)S(1)}, bf16[32,1152]{1,0:T(8,128)(2,1)S(1)}, u32[]{:S(2)}, u32[]{:S(2)}) collective-permute-start(bf16[32,1152]{1,0:T(8,128)(2,1)S(1)} %get-tuple-element.42), channel_id=1, source_target_pairs={{4,20},{12,28},{20,4},{28,12},{5,21},{13,29},{21,5},{29,13},{6,22}... | collective-permute-start | bytes 221192 | tf_op jit(solution)/shard_map/ppermute | solution.py:159
  18.2 2.2 %collective-permute-start.6 = (bf16[32,1024]{1,0:T(8,128)(2,1)S(1)}, bf16[32,1024]{1,0:T(8,128)(2,1)S(1)}, u32[]{:S(2)}, u32[]{:S(2)}) collective-permute-start(bf16[32,1024]{1,0:T(8,128)(2,1)S(1)} %merge_last.1.own_ref), channel_id=1, source_target_pairs={{4,0},{12,8},{20,16},{28,24},{5,1},{13,9},{21,17},{29,25},{6,2},{1... | collective-permute-start | bytes 196616 | tf_op jit(solution)/shard_map/ppermute | solution.py:156
  20.3 2.2 %copy-start.4 = (bf16[4,1024,512]{2,1,0:T(8,128)(2,1)S(1)}, bf16[4,1024,512]{2,1,0:T(8,128)(2,1)}, u32[]{:S(2)}) copy-start(bf16[4,1024,512]{2,1,0:T(8,128)(2,1)} %win_ref.1) | copy-start | bytes 12582916
  22.5 2.2 %copy-start.5 = (bf16[4,512,1024]{2,1,0:T(8,128)(2,1)S(1)}, bf16[4,512,1024]{2,1,0:T(8,128)(2,1)}, u32[]{:S(2)}) copy-start(bf16[4,512,1024]{2,1,0:T(8,128)(2,1)} %wout_ref.1) | copy-start | bytes 12582916
  24.7 13.3 %copy-start = (bf16[2048,1024]{1,0:T(8,128)(2,1)S(1)}, bf16[2048,1024]{1,0:T(8,128)(2,1)}, u32[]{:S(2)}) copy-start(bf16[2048,1024]{1,0:T(8,128)(2,1)} %sp_ref.7) | copy-start | bytes 12582916
  24.7 13.3 %copy-start.3 = (bf16[1024,1024]{1,0:T(8,128)(2,1)S(1)}, bf16[1024,1024]{1,0:T(8,128)(2,1)}, u32[]{:S(2)}) copy-start(bf16[1024,1024]{1,0:T(8,128)(2,1)} %tok_ref.9) | copy-start | bytes 6291460
  26.3 3.3 %collective-permute-start.7 = (bf16[32,1024]{1,0:T(8,128)(2,1)S(1)}, bf16[32,1024]{1,0:T(8,128)(2,1)S(1)}, u32[]{:S(2)}, u32[]{:S(2)}) collective-permute-start(bf16[32,1024]{1,0:T(8,128)(2,1)S(1)} %get-tuple-element.44), channel_id=1, source_target_pairs={{0,4},{8,12},{16,20},{24,28},{1,5},{9,13},{17,21},{25,29},{2,6},{1... | collective-permute-start | bytes 196616 | tf_op jit(solution)/shard_map/ppermute | solution.py:153
  29.6 5.0 %collective-permute-start.8 = (bf16[32,1024]{1,0:T(8,128)(2,1)S(1)}, bf16[32,1024]{1,0:T(8,128)(2,1)S(1)}, u32[]{:S(2)}, u32[]{:S(2)}) collective-permute-start(bf16[32,1024]{1,0:T(8,128)(2,1)S(1)} %fusion), channel_id=1, source_target_pairs={{4,12},{12,4},{20,28},{28,20},{5,13},{13,5},{21,29},{29,21},{6,14}... | collective-permute-start | bytes 196616 | tf_op jit(solution)/shard_map/ppermute | solution.py:159
  34.6 5.0 %collective-permute-start.9 = (bf16[32,1024]{1,0:T(8,128)(2,1)S(1)}, bf16[32,1024]{1,0:T(8,128)(2,1)S(1)}, u32[]{:S(2)}, u32[]{:S(2)}) collective-permute-start(bf16[32,1024]{1,0:T(8,128)(2,1)S(1)} %fusion.1), channel_id=1, source_target_pairs={{4,20},{12,28},{20,4},{28,12},{5,21},{13,29},{21,5},{29,13},{6,22}... | collective-permute-start | bytes 196616 | tf_op jit(solution)/shard_map/ppermute | solution.py:159
  39.7 5.1 %collective-permute-start.10 = (bf16[32,1024]{1,0:T(8,128)(2,1)S(1)}, bf16[32,1024]{1,0:T(8,128)(2,1)S(1)}, u32[]{:S(2)}, u32[]{:S(2)}) collective-permute-start(bf16[32,1024]{1,0:T(8,128)(2,1)S(1)} %add_convert_fusion.refs_0_), channel_id=1, source_target_pairs={{4,5},{5,4},{6,7},{7,6},{12,13},{13,12},{14,15},{15,14},{20,21},{2... | collective-permute-start | bytes 196616 | tf_op jit(solution)/shard_map/ppermute | solution.py:163
  44.8 9.7 %collective-permute-start.11 = (bf16[64,1024]{1,0:T(8,128)(2,1)S(1)}, bf16[64,1024]{1,0:T(8,128)(2,1)S(1)}, u32[]{:S(2)}, u32[]{:S(2)}) collective-permute-start(bf16[64,1024]{1,0:T(8,128)(2,1)S(1)} %pad_maximum_fusion), channel_id=1, source_target_pairs={{4,6},{5,7},{6,4},{7,5},{12,14},{13,15},{14,12},{15,13},{20,22},{2... | collective-permute-start | bytes 393224 | tf_op jit(solution)/shard_map/ppermute | solution.py:163
  50.7 2.2 %copy-start.1 = (bf16[2048,1024]{1,0:T(8,128)(2,1)S(1)}, bf16[2048,1024]{1,0:T(8,128)(2,1)}, u32[]{:S(2)}) copy-start(bf16[2048,1024]{1,0:T(8,128)(2,1)} %sp_ref.7) | copy-start | bytes 12582916
  54.5 10.0 %collective-permute-start.14 = (bf16[64,1024]{1,0:T(8,128)(2,1)S(1)}, bf16[64,1024]{1,0:T(8,128)(2,1)S(1)}, u32[]{:S(2)}, u32[]{:S(2)}) collective-permute-start(bf16[64,1024]{1,0:T(8,128)(2,1)S(1)} %collective-permute-done.11.refs_2_), channel_id=1, source_target_pairs={{4,0},{12,8},{20,16},{28,24},{5,1},{13,9},{21,17},{29,25},{6,2},{1... | collective-permute-start | bytes 393224 | tf_op jit(solution)/shard_map/ppermute | solution.py:156
  55.8 5.2 %collective-permute-start.2 = (f32[40,256]{1,0:T(8,128)S(1)}, f32[40,256]{1,0:T(8,128)S(1)}, u32[]{:S(2)}, u32[]{:S(2)}) collective-permute-start(f32[40,256]{1,0:T(8,128)S(1)} %get-tuple-element.45), channel_id=1, source_target_pairs={{0,3},{1,2},{2,1},{3,0},{4,7},{5,6},{6,5},{7,4},{8,11},{9,10},{10,... | collective-permute-start | bytes 122888 | tf_op jit(solution)/shard_map/ppermute | solution.py:205
  58.0 6.5 %collective-permute-start.12 = (bf16[32,1024]{1,0:T(8,128)(2,1)S(1)}, bf16[32,1024]{1,0:T(8,128)(2,1)S(1)}, u32[]{:S(2)}, u32[]{:S(2)}) collective-permute-start(bf16[32,1024]{1,0:T(8,128)(2,1)S(1)} %add_convert_fusion.refs_0_), channel_id=1, source_target_pairs={{4,0},{12,8},{20,16},{28,24},{5,1},{13,9},{21,17},{29,25},{6,2},{1... | collective-permute-start | bytes 196616 | tf_op jit(solution)/shard_map/ppermute | solution.py:156
  59.3 5.3 %collective-permute-start.13 = (bf16[32,1024]{1,0:T(8,128)(2,1)S(1)}, bf16[32,1024]{1,0:T(8,128)(2,1)S(1)}, u32[]{:S(2)}, u32[]{:S(2)}) collective-permute-start(bf16[32,1024]{1,0:T(8,128)(2,1)S(1)} %collective-permute-done.10.refs_1_), channel_id=1, source_target_pairs={{4,0},{12,8},{20,16},{28,24},{5,1},{13,9},{21,17},{29,25},{6,2},{1... | collective-permute-start | bytes 196616 | tf_op jit(solution)/shard_map/ppermute | solution.py:156
  60.6 3.8 %collective-permute-start.1 = (f32[40,256]{1,0:T(8,128)S(1)}, f32[40,256]{1,0:T(8,128)S(1)}, u32[]{:S(2)}, u32[]{:S(2)}) collective-permute-start(f32[40,256]{1,0:T(8,128)S(1)} %get-tuple-element.46), channel_id=1, source_target_pairs={{0,2},{1,3},{2,0},{3,1},{4,6},{5,7},{6,4},{7,5},{8,10},{9,11},{10,... | collective-permute-start | bytes 122888 | tf_op jit(solution)/shard_map/ppermute | solution.py:205
  61.1 3.3 %collective-permute-start = (f32[40,256]{1,0:T(8,128)S(1)}, f32[40,256]{1,0:T(8,128)S(1)}, u32[]{:S(2)}, u32[]{:S(2)}) collective-permute-start(f32[40,256]{1,0:T(8,128)S(1)} %get-tuple-element.47), channel_id=1, source_target_pairs={{0,1},{1,0},{2,3},{3,2},{4,5},{5,4},{6,7},{7,6},{8,9},{9,8},{10,11... | collective-permute-start | bytes 122888 | tf_op jit(solution)/shard_map/ppermute | solution.py:205

commit v2 on v0

v2 whole, which is shorter than its diff:
```python
import functools

import jax
import jax.numpy as jnp
from jax import lax
from jax.experimental import pallas as pl
from jax.experimental.pallas import tpu as pltpu
from jax.sharding import PartitionSpec as P

P_SIZE = 8
LANES = 128
TOKEN_CHUNKS = 4
BF = jnp.bfloat16
F32 = jnp.float32
VMEM = pl.BlockSpec(memory_space=pltpu.VMEM)
HBM = pl.BlockSpec(memory_space=pltpu.HBM)
MIB = 1 << 20
KERNEL_BYTES = 105 * MIB // 2


def sds(shape, dtype):
    return jax.ShapeDtypeStruct(shape, dtype)


def call(kernel, outs, in_specs, name, flops=0, moved=0, vmem=2 * MIB, **kw):
    return pl.pallas_call(
        kernel,
        out_shape=outs,
        in_specs=in_specs,
        out_specs=jax.tree.map(lambda _: VMEM, outs),
        name=name,
        compiler_params=pltpu.CompilerParams(vmem_limit_bytes=vmem),
        cost_estimate=pl.CostEstimate(flops=flops, bytes_accessed=moved, transcendentals=0),
        **kw,
    )


def lane_pack(rows, *columns):
    lane = lax.broadcasted_iota(jnp.int32, (rows, LANES), 1)
    out = jnp.zeros((rows, LANES), F32)
    for k, column in enumerate(columns):
        out = jnp.where(lane == k, column, out)
    return out


def write_state(num, top, tot, num_ref, st_ref, msg_ref):
    rows, d = num.shape
    num_ref[...] = num
    st_ref[...] = lane_pack(rows, top, tot)
    hi = tot.astype(BF).astype(F32)
    lo = (tot - hi).astype(BF).astype(F32)
    msg_ref[:, :d] = num.astype(BF)
    msg_ref[:, d:] = lane_pack(rows, top, hi, lo).astype(BF)


def dot_t(a, b):
    return lax.dot_general(a, b, (((1,), (1,)), ((), ())), preferred_element_type=F32)


def dispatch_kernel(chunks, sp_hbm, tok_hbm, tok_ref, flight_ref, num_ref, st_ref, msg_ref, sp_ref, sems):
    rows = flight_ref.shape[0]
    n = tok_ref.shape[0]
    step = n // chunks
    first = pltpu.make_async_copy(sp_hbm.at[pl.ds(0, rows)], sp_ref, sems.at[chunks])
    first.start()
    copies = []
    for c in range(chunks):
        part = pl.ds(c * step, step)
        copy = pltpu.make_async_copy(tok_hbm.at[part], tok_ref.at[part], sems.at[c])
        copy.start()
        copies.append(copy)
    first.wait()
    sp = sp_ref[...]
    for c, copy in enumerate(copies):
        copy.wait()
        flight_ref[:, c * step : (c + 1) * step] = dot_t(sp, tok_ref[c * step : (c + 1) * step, :])
    flight = flight_ref[...]
    top = jnp.max(flight, axis=1, keepdims=True).astype(BF).astype(F32)
    e = jnp.exp(flight - top)
    tot = jnp.sum(e, axis=1, keepdims=True)
    num = jnp.dot(e.astype(BF), tok_ref[...], preferred_element_type=F32)
    write_state(num, top, tot, num_ref, st_ref, msg_ref)


def merge(num_ref, st_ref, recvs):
    d = num_ref.shape[1]
    rs = [r[:, d:].astype(F32) for r in recvs]
    tops = [st_ref[:, 0:1]] + [r[:, 0:1] for r in rs]
    tots = [st_ref[:, 1:2]] + [r[:, 1:2] + r[:, 2:3] for r in rs]
    new = functools.reduce(jnp.maximum, tops)
    scales = [jnp.exp(t - new) for t in tops]
    num = num_ref[...] * scales[0]
    for r, s in zip(recvs, scales[1:]):
        num = num + r[:, :d].astype(F32) * s
    return num, new, sum(t * s for t, s in zip(tots, scales))


def merge_kernel(count, *refs):
    num_ref, st_ref, recvs, outs = refs[0], refs[1], refs[2 : 2 + count], refs[2 + count :]
    write_state(*merge(num_ref, st_ref, recvs), *outs)


def merge_last_kernel(*refs):
    num_ref, st_ref, recvs, out_ref = refs[0], refs[1], refs[2:-1], refs[-1]
    num, _, tot = merge(num_ref, st_ref, recvs)
    out_ref[...] = (num / tot).astype(BF)


def mlp_kernel(sizes, x_ref, win_ref, wout_ref, keep_ref, send_ref):
    x = x_ref[...].astype(F32)
    experts = win_ref.shape[0]
    width = keep_ref.shape[1]
    right = half_of(*sizes) == 1
    sent = []
    for e in range(experts):
        rows = slice(e * P_SIZE, (e + 1) * P_SIZE)
        pre = jnp.dot(x[rows].astype(BF), win_ref[e], preferred_element_type=F32)
        hidden = jax.nn.gelu(pre).astype(BF)
        out = jnp.dot(hidden, wout_ref[e], preferred_element_type=F32)
        a, b = out[:, :width], out[:, width:]
        keep_ref[rows, :] = jnp.where(right, b, a)
        sent.append(jnp.where(right, a, b))
    send_ref[...] = jnp.concatenate(sent, axis=0).astype(BF)


def add_kernel(*refs):
    keep_ref, recvs, (sum_ref, msg_ref) = refs[0], refs[1:-2], refs[-2:]
    total = keep_ref[...]
    for r in recvs:
        total = total + r[...].astype(F32)
    sum_ref[...] = total
    msg_ref[...] = total.astype(BF)


def stats_kernel(start, stop, step, sp_ref, tok_ref, *refs):
    n = tok_ref.shape[0]
    mo_ref, lo_ref = refs[-2:]
    if start == 0:
        m, l = jnp.full((8, n), -jnp.inf, F32), jnp.zeros((8, n), F32)
    else:
        m, l = refs[0][...], refs[1][...]
    tok = tok_ref[...]
    for r in range(start, stop, step):
        x = dot_t(sp_ref[r : r + step, :], tok).reshape(step // 8, 8, n)
        new = jnp.maximum(m, jnp.max(x, axis=0))
        l = l * jnp.exp(m - new) + jnp.sum(jnp.exp(x - new[None]), axis=0)
        m = new
    mo_ref[...] = m
    lo_ref[...] = l


def pack_kernel(flight_ref, m_ref, l_ref, out_ref):
    rows = flight_ref.shape[0]
    m, l = m_ref[...], l_ref[...]
    top = jnp.max(m, axis=0, keepdims=True)
    tot = jnp.sum(l * jnp.exp(m - top), axis=0, keepdims=True)
    sub = lax.broadcasted_iota(jnp.int32, m.shape, 0)
    tail = jnp.where(sub == 0, top, jnp.where(sub == 1, tot, 0.0))
    blocks, _, share = out_ref.shape
    for b in range(blocks):
        out_ref[b, :rows, :] = flight_ref[:, b * share : (b + 1) * share]
        out_ref[b, rows:, :] = tail[:, b * share : (b + 1) * share]


def weights_kernel(parts_ref, out_ref):
    blocks, rows, _ = parts_ref.shape
    rows -= 8
    tops = [parts_ref[b, rows : rows + 1, :] for b in range(blocks)]
    top = functools.reduce(jnp.maximum, tops)
    tot = sum(parts_ref[b, rows + 1 : rows + 2, :] * jnp.exp(t - top) for b, t in enumerate(tops))
    me = lax.axis_index("slot")
    w = [jnp.exp(parts_ref[me ^ k, :rows, :] - top) / tot for k in range(blocks)]
    out_ref[...] = jnp.concatenate(w, axis=0).T.astype(BF)


def combine_kernel(sizes, w_ref, mine_ref, recv_ref, out_ref):
    right = half_of(*sizes) == 1
    mine, recv = mine_ref[...], recv_ref[...]
    width = mine.shape[1]
    w = w_ref[...]
    out_ref[:, :width] = jnp.dot(w, jnp.where(right, recv, mine), preferred_element_type=F32).astype(BF)
    out_ref[:, width:] = jnp.dot(w, jnp.where(right, mine, recv), preferred_element_type=F32).astype(BF)


def half_of(n_tok, n_slot):
    bits = [lax.axis_index("tok") >> k for k in range(n_tok.bit_length() - 1)]
    bits += [lax.axis_index("slot") >> k for k in range(n_slot.bit_length() - 1)]
    return functools.reduce(lambda a, b: a ^ b, bits) & 1


def masks(bits):
    groups = []
    for at in range(0, len(bits), 2):
        pair = bits[at : at + 2]
        groups.append([pair[0]] if len(pair) == 1 else [pair[0], pair[1], pair[0] | pair[1]])
    return groups


def body(n_tok, n_slot, tokens, slot_params, w_in, w_out):
    n, d = tokens.shape
    experts, _, h = w_in.shape
    slots = slot_params.shape[0]
    rows = experts * P_SIZE
    width = d // 2
    share = n // n_slot
    def swap(x, tok, slot=0):
        pairs = [(i * n_slot + j, (i ^ tok) * n_slot + (j ^ slot)) for i in range(n_tok) for j in range(n_slot)]
        return lax.ppermute(x, ("tok", "slot"), pairs)

    def odd(mask):
        return mask.bit_count() & 1

    tok_groups = masks([1 << b for b in range(1, n_tok.bit_length() - 1)])
    slot_groups = masks([1 << b for b in range(n_slot.bit_length() - 1)])

    pieces = {"state": (), "at": 0}

    def stats(anchor, count):
        start, stop = pieces["at"], min(slots, pieces["at"] + count)
        if start == stop:
            return anchor
        *state, anchor = lax.optimization_barrier((*pieces["state"], anchor))
        state = call(
            functools.partial(stats_kernel, start, stop, min(256, stop - start)),
            [sds((8, n), F32)] * 2,
            [VMEM] * (2 + len(state)),
            "stats",
            flops=2 * (stop - start) * n * d,
            moved=4 * MIB,
            vmem=12 * MIB,
        )(slot_params, tok_v, *state)
        pieces.update(state=tuple(state), at=stop)
        return anchor

    def meet(values):
        k = len(pieces["state"])
        out = lax.optimization_barrier((*pieces["state"], *values))
        pieces.update(state=tuple(out[:k]))
        return list(out[k:])

    state = [sds((rows, d), F32), sds((rows, LANES), F32), sds((rows, d + LANES), BF)]
    chunks = TOKEN_CHUNKS
    tok_v, flight, num, st, msg = call(
        functools.partial(dispatch_kernel, chunks),
        [sds((n, d), BF), sds((rows, n), F32)] + state,
        [HBM, HBM],
        "dispatch",
        flops=4 * rows * n * d,
        moved=8 * MIB,
        vmem=KERNEL_BYTES - 2 * n * d,
        scratch_shapes=[pltpu.VMEM((rows, d), BF), pltpu.SemaphoreType.DMA((chunks + 1,))],
    )(slot_params, tokens)
    recvs = [swap(msg, 1)]
    msg = stats(msg, 256)
    for group in tok_groups:
        recvs = meet(recvs)
        num, st, msg = call(
            functools.partial(merge_kernel, len(recvs)), state, [VMEM] * (2 + len(recvs)), "merge", moved=8 * MIB
        )(num, st, *recvs)
        recvs = [swap(msg, mask | 1) for mask in group]
        msg = stats(msg, 768)
    recvs = meet(recvs)
    slot_in = call(merge_last_kernel, sds((rows, d), BF), [VMEM] * (2 + len(recvs)), "merge_last", moved=8 * MIB)(
        num, st, *recvs
    )

    def add(keep, recvs):
        outs = [sds((rows, width), F32), sds((rows, width), BF)]
        return call(add_kernel, outs, [VMEM] * (1 + len(recvs)), "add", moved=8 * MIB)(keep, *recvs)

    keep, send = call(
        functools.partial(mlp_kernel, (n_tok, n_slot)),
        [sds((rows, width), F32), sds((rows, width), BF)],
        [VMEM] * 3,
        "mlp",
        flops=4 * rows * d * h,
        moved=8 * MIB,
        vmem=4 * MIB,
    )(slot_in, w_in, w_out)
    recvs = [swap(send, 1)]
    send = stats(send, 256)
    for group in tok_groups:
        recvs = meet(recvs)
        keep, msg = add(keep, recvs)
        recvs = [swap(msg, mask | odd(mask)) for mask in group]
        msg = stats(msg, 768)
    stats(msg, slots)
    recvs = meet(recvs)
    _, msg = add(keep, recvs)
    outs = [msg]

    pack = call(pack_kernel, sds((n_slot, rows + 8, share), F32), [VMEM] * 3, "pack", moved=MIB)(
        flight, *pieces["state"]
    )
    parts = lax.all_to_all(pack, "slot", split_axis=0, concat_axis=0, tiled=True)
    weights = call(weights_kernel, sds((share, n_slot * rows), BF), [VMEM], "weights", vmem=4 * MIB)(
        parts
    )

    for group in slot_groups:
        have = outs[0] if len(outs) == 1 else jnp.concatenate(outs, axis=0)
        outs = [have] + [swap(have, odd(mask), mask) for mask in group]
    mine = jnp.concatenate(outs, axis=0)
    recv = swap(mine, 1)
    kernel = functools.partial(combine_kernel, (n_tok, n_slot))
    return call(kernel, sds((share, d), BF), [VMEM] * 3, "combine", vmem=8 * MIB)(weights, mine, recv)


def solution(mesh):
    sizes = dict(mesh.shape)
    return jax.shard_map(
        functools.partial(body, sizes["tok"], sizes["slot"]),
        mesh=mesh,
        in_specs=(P("tok", None), P("slot", None), P("slot", None, "tok"), P("slot", "tok", None)),
        out_specs=P(("tok", "slot"), None),
        check_vma=False,
    )
```

time: 139 us -> 40.9 us (0.29)
  blocking collectives: 85.1 us -> 0 us
  matrix products: 14.3 us -> 0 us
  starting transfers between devices: 3.29 us -> 17.3 us
  Pallas kernels: 0 us -> 13.7 us
  between operations: 13.4 us -> 0.15 us
  other arithmetic: 5.79 us -> 0 us
  local copies, waits for them, and re-layouts: 5.43 us -> 0.03 us
  waiting for transfers between devices: 11.1 us -> 9.56 us
    psum x3 -> x0, blocking collectives: 43.7 us -> none  [the longest x1 23.4 us: body(): slot_out = lax.psum(partial_out, 'tok').astype(jnp.bfloat16)]
    pmax x2 -> x0, blocking collectives: 27.1 us -> none  [the longest x1 15.2 us: body(): col_max = lax.pmax(jnp.max(flight, axis=1), 'tok')]
    all_gather x1 -> x0, blocking collectives: 14.3 us -> none  [body(): all_outputs = lax.all_gather(slot_out, 'slot', axis=0, tiled=True)]
    dot_general x4 -> x0, matrix products: 14.3 us -> none  [the longest x1 6.38 us: body(): lax.dot_general(slot_params, tokens, (((1,), (1,)), ((), ())), preferred_...]
    pallas_call x0 -> x13, Pallas kernels: none -> 13.7 us  [the longest x4 5.85 us: stats(): call(functools.partial(stats_kernel, start, stop, min(256, stop - start))...]
    ppermute x0 -> x12, starting transfers between devices: none -> 12.4 us  [swap(): return lax.ppermute(x, ('tok', 'slot'), pairs)]
    psum x1 -> x0, waiting for transfers between devices: 11.1 us -> none  [body(): numer, totals = lax.psum((numer, jnp.sum(dispatch_exp, axis=1)), 'tok')]
    all_to_all x1, waiting for transfers between devices: 0.01 us -> 6.65 us  [body(): lax.all_to_all(pack, 'slot', split_axis=0, concat_axis=0, tiled=True)]
  transfers between devices with their start and end apart: 2 -> 13, of which waited for: 1 -> 7; matrix products, arithmetic and copies ran while one was open for 8% -> 0% of each run, Pallas kernels for 0% -> 16%
where the time goes in v2:
time: 40.9 us; the launch traced here: 40.7 us
  starting transfers between devices  17.3 us (42%)
  Pallas kernels  13.7 us (33%)
  waiting for transfers between devices  9.56 us (23%)
    ppermute x12, starting transfers between devices, swap(): return lax.ppermute(x, ('tok', 'slot'), pairs)  12.4 us
    all_to_all x1, waiting for transfers between devices, body(): lax.all_to_all(pack, 'slot', split_axis=0, concat_axis=0, tiled=True)  6.65 us
    pallas_call x4, Pallas kernels, stats(): call(functools.partial(stats_kernel, start, stop, min(256, stop - start))...  5.85 us
    all_to_all x1, starting transfers between devices, body(): lax.all_to_all(pack, 'slot', split_axis=0, concat_axis=0, tiled=True)  4.86 us
    pallas_call x1, Pallas kernels, body(): call(functools.partial(dispatch_kernel, chunks), [sds((n, d), BF), sds((r...  3.36 us
    ppermute x12, waiting for transfers between devices, swap(): return lax.ppermute(x, ('tok', 'slot'), pairs)  2.91 us
    pallas_call x1, Pallas kernels, body(): call(functools.partial(mlp_kernel, (n_tok, n_slot)), [sds((rows, width),...  1.54 us
    pallas_call x1, Pallas kernels, body(): call(kernel, sds((share, d), BF), [VMEM] * 3, 'combine', vmem=8 * MIB)  1.09 us
  transfers between devices with their start and end apart: 13, of which 7 were waited for; matrix products, arithmetic and copies ran while one was open for 0% of the time, Pallas kernels for 16%

profile of v2, /device:TPU:0, one launch (start us, length us, event | category | flops | bytes accessed | tf_op | source)
XLA Modules:
  0.0 40.7 jit_solution(10283140956572723461)
XLA Ops:
  0.0 0.0 copy-start
  0.0 3.4 %dispatch.1 = (bf16[1024,1024]{1,0:T(8,128)(2,1)S(1)}, f32[32,1024]{1,0:T(8,128)S(1)}, f32[32,1024]{1,0:T(8,128)S(1)}, f32[32,128]{1,0:T(8,128)S(1)}, bf16[32,1152]{1,0:T(8,128)(2,1)S(1)}) custom-call(bf16[2048,1024]{1,0:T(8,128)(2,1)} %sp_ref.7, bf16[1024,1024]{1,0:T(8,128)(2,1)} %tok_hbm.1), custom_call_target="tpu_custom_call" | custom-call | flops 134217728 | bytes 8388608 | tf_op jit(solution)/shard_map/dispatch/pallas_call | solution.py:243
  3.4 0.6 %collective-permute-start = (bf16[32,1152]{1,0:T(8,128)(2,1)S(1)}, bf16[32,1152]{1,0:T(8,128)(2,1)S(1)}, u32[]{:S(2)}, u32[]{:S(2)}) collective-permute-start(bf16[32,1152]{1,0:T(8,128)(2,1)S(1)} %get-tuple-element.52), channel_id=1, source_target_pairs={{0,4},{1,5},{2,6},{3,7},{4,0},{5,1},{6,2},{7,3},{8,12},{9,13},{10,... | collective-permute-start | bytes 221192 | tf_op jit(solution)/shard_map/ppermute | solution.py:208
  3.9 0.0 copy-done
  3.9 0.0 copy-start.2
  3.9 0.9 %stats.4 = (f32[8,1024]{1,0:T(8,128)S(1)}, f32[8,1024]{1,0:T(8,128)S(1)}) custom-call(bf16[2048,1024]{1,0:T(8,128)(2,1)S(1)} %copy-done, bf16[1024,1024]{1,0:T(8,128)(2,1)S(1)} %get-tuple-element.49.tok_ref), custom_call_target="tpu_custom_call" | custom-call | flops 536870912 | bytes 4194304 | tf_op jit(solution)/shard_map/stats/pallas_call | solution.py:223
  4.9 0.0 copy-start.1
  4.9 0.0 collective-permute-done.refs_2_
  4.9 0.2 merge.1
  5.0 3.6 %collective-permute-start.3 = (bf16[32,1152]{1,0:T(8,128)(2,1)S(1)}, bf16[32,1152]{1,0:T(8,128)(2,1)S(1)}, u32[]{:S(2)}, u32[]{:S(2)}) collective-permute-start(bf16[32,1152]{1,0:T(8,128)(2,1)S(1)} %get-tuple-element.58), channel_id=1, source_target_pairs={{0,28},{1,29},{2,30},{3,31},{4,24},{5,25},{6,26},{7,27},{8,20},{9,... | collective-permute-start | bytes 221192 | tf_op jit(solution)/shard_map/ppermute | solution.py:208
  8.7 0.4 %collective-permute-start.2 = (bf16[32,1152]{1,0:T(8,128)(2,1)S(1)}, bf16[32,1152]{1,0:T(8,128)(2,1)S(1)}, u32[]{:S(2)}, u32[]{:S(2)}) collective-permute-start(bf16[32,1152]{1,0:T(8,128)(2,1)S(1)} %get-tuple-element.58), channel_id=1, source_target_pairs={{0,20},{1,21},{2,22},{3,23},{4,16},{5,17},{6,18},{7,19},{8,28},{9,... | collective-permute-start | bytes 221192 | tf_op jit(solution)/shard_map/ppermute | solution.py:208
  9.1 0.1 collective-permute-start.1
  9.2 2.0 %stats.5 = (f32[8,1024]{1,0:T(8,128)S(1)}, f32[8,1024]{1,0:T(8,128)S(1)}) custom-call(bf16[2048,1024]{1,0:T(8,128)(2,1)S(1)} %copy-done, bf16[1024,1024]{1,0:T(8,128)(2,1)S(1)} %get-tuple-element.49.tok_ref, f32[8,1024]{1,0:T(8,128)S(1)} %get-tuple-element.59.refs_0_, f32[8,1024]{1,0:T(8,128)S(1)} %get-tuple-element.60.refs_1_), custom_call_target="tpu_custom_call" | custom-call | flops 1610612736 | bytes 4194304 | tf_op jit(solution)/shard_map/stats/pallas_call | solution.py:223
  11.2 0.1 collective-permute-done.3.refs_4_
  11.4 1.4 %collective-permute-done.2.refs_3_ = bf16[32,1152]{1,0:T(8,128)(2,1)S(1)} collective-permute-done((bf16[32,1152]{1,0:T(8,128)(2,1)S(1)}, bf16[32,1152]{1,0:T(8,128)(2,1)S(1)}, u32[]{:S(2)}, u32[]{:S(2)}) %collective-permute-start.2) | collective-permute-done | bytes 73760 | tf_op jit(solution)/shard_map/ppermute | solution.py:208
  12.7 0.5 %collective-permute-done.1.refs_2_ = bf16[32,1152]{1,0:T(8,128)(2,1)S(1)} collective-permute-done((bf16[32,1152]{1,0:T(8,128)(2,1)S(1)}, bf16[32,1152]{1,0:T(8,128)(2,1)S(1)}, u32[]{:S(2)}, u32[]{:S(2)}) %collective-permute-start.1) | collective-permute-done | bytes 73760 | tf_op jit(solution)/shard_map/ppermute | solution.py:208
  13.3 0.2 merge_last.1.x_ref
  13.5 0.0 copy-done.2
  13.5 0.0 copy-done.1
  13.5 1.5 %mlp.1 = (f32[32,512]{1,0:T(8,128)S(1)}, bf16[32,512]{1,0:T(8,128)(2,1)S(1)}) custom-call(bf16[32,1024]{1,0:T(8,128)(2,1)S(1)} %merge_last.1.x_ref, bf16[4,1024,512]{2,1,0:T(8,128)(2,1)S(1)} %copy-done.1, bf16[4,512,1024]{2,1,0:T(8,128)(2,1)S(1)} %copy-done.2), custom_call_target="tpu_custom_call" | custom-call | flops 67108864 | bytes 8388608 | tf_op jit(solution)/shard_map/mlp/pallas_call | solution.py:271
  15.0 0.2 collective-permute-start.4
  15.3 0.9 %stats.6 = (f32[8,1024]{1,0:T(8,128)S(1)}, f32[8,1024]{1,0:T(8,128)S(1)}) custom-call(bf16[2048,1024]{1,0:T(8,128)(2,1)S(1)} %copy-done, bf16[1024,1024]{1,0:T(8,128)(2,1)S(1)} %get-tuple-element.49.tok_ref, f32[8,1024]{1,0:T(8,128)S(1)} %get-tuple-element.71.refs_0_, f32[8,1024]{1,0:T(8,128)S(1)} %get-tuple-element.72.refs_1_), custom_call_target="tpu_custom_call" | custom-call | flops 536870912 | bytes 4194304 | tf_op jit(solution)/shard_map/stats/pallas_call | solution.py:223
  16.2 0.1 collective-permute-done.4.refs_1_
  16.3 1.6 %collective-permute-start.7 = (bf16[32,512]{1,0:T(8,128)(2,1)S(1)}, bf16[32,512]{1,0:T(8,128)(2,1)S(1)}, u32[]{:S(2)}, u32[]{:S(2)}) collective-permute-start(bf16[32,512]{1,0:T(8,128)(2,1)S(1)} %get-tuple-element.79), channel_id=1, source_target_pairs={{0,24},{1,25},{2,26},{3,27},{4,28},{5,29},{6,30},{7,31},{8,16},{9,... | collective-permute-start | bytes 98312 | tf_op jit(solution)/shard_map/ppermute | solution.py:208
  17.9 1.2 %collective-permute-start.6 = (bf16[32,512]{1,0:T(8,128)(2,1)S(1)}, bf16[32,512]{1,0:T(8,128)(2,1)S(1)}, u32[]{:S(2)}, u32[]{:S(2)}) collective-permute-start(bf16[32,512]{1,0:T(8,128)(2,1)S(1)} %get-tuple-element.79), channel_id=1, source_target_pairs={{0,20},{1,21},{2,22},{3,23},{4,16},{5,17},{6,18},{7,19},{8,28},{9,... | collective-permute-start | bytes 98312 | tf_op jit(solution)/shard_map/ppermute | solution.py:208
  19.0 0.5 %collective-permute-start.5 = (bf16[32,512]{1,0:T(8,128)(2,1)S(1)}, bf16[32,512]{1,0:T(8,128)(2,1)S(1)}, u32[]{:S(2)}, u32[]{:S(2)}) collective-permute-start(bf16[32,512]{1,0:T(8,128)(2,1)S(1)} %get-tuple-element.79), channel_id=1, source_target_pairs={{0,12},{1,13},{2,14},{3,15},{4,8},{5,9},{6,10},{7,11},{8,4},{9,5},... | collective-permute-start | bytes 98312 | tf_op jit(solution)/shard_map/ppermute | solution.py:208
  19.6 2.0 %stats.7 = (f32[8,1024]{1,0:T(8,128)S(1)}, f32[8,1024]{1,0:T(8,128)S(1)}) custom-call(bf16[2048,1024]{1,0:T(8,128)(2,1)S(1)} %copy-done, bf16[1024,1024]{1,0:T(8,128)(2,1)S(1)} %get-tuple-element.49.tok_ref, f32[8,1024]{1,0:T(8,128)S(1)} %get-tuple-element.80.refs_0_, f32[8,1024]{1,0:T(8,128)S(1)} %get-tuple-element.81.refs_1_), custom_call_target="tpu_custom_call" | custom-call | flops 1610612736 | bytes 4194304 | tf_op jit(solution)/shard_map/stats/pallas_call | solution.py:223
  21.6 0.0 collective-permute-done.7.refs_3_
  21.6 0.3 collective-permute-done.6.refs_2_
  21.9 0.5 %collective-permute-done.5.refs_1_ = bf16[32,512]{1,0:T(8,128)(2,1)S(1)} collective-permute-done((bf16[32,512]{1,0:T(8,128)(2,1)S(1)}, bf16[32,512]{1,0:T(8,128)(2,1)S(1)}, u32[]{:S(2)}, u32[]{:S(2)}) %collective-permute-start.5) | collective-permute-done | bytes 32800 | tf_op jit(solution)/shard_map/ppermute | solution.py:208
  22.4 0.6 %add.3 = (f32[32,512]{1,0:T(8,128)}, bf16[32,512]{1,0:T(8,128)(2,1)S(1)}) custom-call(f32[32,512]{1,0:T(8,128)S(1)} %get-tuple-element.86.refs_0_, bf16[32,512]{1,0:T(8,128)(2,1)S(1)} %collective-permute-done.5.refs_1_, bf16[32,512]{1,0:T(8,128)(2,1)S(1)} %collective-permute-done.6.refs_2_, bf16[32,512]{1,0:T(8,128)(2,1)S(1)} %collective-permute-done.7.refs_3_), custom_call_target="tpu_custom_call" | custom-call | bytes 8388608 | tf_op jit(solution)/shard_map/add/pallas_call | solution.py:269
  23.0 3.6 %collective-permute-start.10 = (bf16[32,512]{1,0:T(8,128)(2,1)S(1)}, bf16[32,512]{1,0:T(8,128)(2,1)S(1)}, u32[]{:S(2)}, u32[]{:S(2)}) collective-permute-start(bf16[32,512]{1,0:T(8,128)(2,1)S(1)} %get-tuple-element.90), channel_id=1, source_target_pairs={{0,3},{1,2},{2,1},{3,0},{4,7},{5,6},{6,5},{7,4},{8,11},{9,10},{10,... | collective-permute-start | bytes 98312 | tf_op jit(solution)/shard_map/ppermute | solution.py:208
  26.6 0.0 collective-permute-start.9
  26.6 0.5 %collective-permute-start.8 = (bf16[32,512]{1,0:T(8,128)(2,1)S(1)}, bf16[32,512]{1,0:T(8,128)(2,1)S(1)}, u32[]{:S(2)}, u32[]{:S(2)}) collective-permute-start(bf16[32,512]{1,0:T(8,128)(2,1)S(1)} %get-tuple-element.90), channel_id=1, source_target_pairs={{0,5},{1,4},{2,7},{3,6},{4,1},{5,0},{6,3},{7,2},{8,13},{9,12},{10,... | collective-permute-start | bytes 98312 | tf_op jit(solution)/shard_map/ppermute | solution.py:208
  27.1 0.7 %pack.1 = f32[4,40,256]{2,1,0:T(8,128)} custom-call(f32[32,1024]{1,0:T(8,128)S(1)} %get-tuple-element.48.flight_ref, f32[8,1024]{1,0:T(8,128)S(1)} %get-tuple-element.84.m_ref, f32[8,1024]{1,0:T(8,128)S(1)} %get-tuple-element.85.l_ref), custom_call_target="tpu_custom_call" | custom-call | bytes 1048576 | tf_op jit(solution)/shard_map/pack/pallas_call | solution.py:292
  27.8 4.9 %all-to-all-start = ((f32[4,40,256]{2,1,0:T(8,128)}), f32[4,40,256]{2,1,0:T(8,128)S(1)}, u32[]{:S(2)}, u32[]{:S(2)}) async-start(f32[4,40,256]{2,1,0:T(8,128)} %pack.1), calls=%async_computation | async-start | bytes 327680 | tf_op jit(solution)/shard_map/all_to_all | solution.py:295
  32.7 0.0 collective-permute-done.8
  32.7 0.0 collective-permute-done.9
  32.7 0.0 collective-permute-done.10
  32.7 0.1 collective-permute-start.11
  32.8 6.7 %all-to-all-done.parts_ref = f32[4,40,256]{2,1,0:T(8,128)S(1)} async-done(((f32[4,40,256]{2,1,0:T(8,128)}), f32[4,40,256]{2,1,0:T(8,128)S(1)}, u32[]{:S(2)}, u32[]{:S(2)}) %all-to-all-start) | async-done | bytes 163872 | tf_op jit(solution)/shard_map/all_to_all | solution.py:295
  39.5 0.1 weights.1.w_ref
  39.6 0.0 collective-permute-done.11.recv_ref
  39.6 1.1 %combine.1 = bf16[256,1024]{1,0:T(8,128)(2,1)} custom-call(bf16[256,128]{1,0:T(8,128)(2,1)S(1)} %weights.1.w_ref, bf16[128,512]{1,0:T(8,128)(2,1)S(1)} %constant_dynamic-update-slice_fusion.mine_ref, bf16[128,512]{1,0:T(8,128)(2,1)S(1)} %collective-permute-done.11.recv_ref), custom_call_target="tpu_custom_call" | custom-call | tf_op jit(solution)/shard_map/combine/pallas_call | solution.py:306
  (5 shorter events, 0.0 us)
Async XLA Ops:
  0.0 3.9 %copy-start = (bf16[2048,1024]{1,0:T(8,128)(2,1)S(1)}, bf16[2048,1024]{1,0:T(8,128)(2,1)}, u32[]{:S(2)}) copy-start(bf16[2048,1024]{1,0:T(8,128)(2,1)} %sp_ref.7) | copy-start | bytes 12582916
  3.4 1.5 %collective-permute-start = (bf16[32,1152]{1,0:T(8,128)(2,1)S(1)}, bf16[32,1152]{1,0:T(8,128)(2,1)S(1)}, u32[]{:S(2)}, u32[]{:S(2)}) collective-permute-start(bf16[32,1152]{1,0:T(8,128)(2,1)S(1)} %get-tuple-element.52), channel_id=1, source_target_pairs={{0,4},{1,5},{2,6},{3,7},{4,0},{5,1},{6,2},{7,3},{8,12},{9,13},{10,... | collective-permute-start | bytes 221192 | tf_op jit(solution)/shard_map/ppermute | solution.py:208
  3.9 9.5 %copy-start.2 = (bf16[4,512,1024]{2,1,0:T(8,128)(2,1)S(1)}, bf16[4,512,1024]{2,1,0:T(8,128)(2,1)}, u32[]{:S(2)}) copy-start(bf16[4,512,1024]{2,1,0:T(8,128)(2,1)} %wout_ref.1) | copy-start | bytes 12582916
  4.9 8.6 %copy-start.1 = (bf16[4,1024,512]{2,1,0:T(8,128)(2,1)S(1)}, bf16[4,1024,512]{2,1,0:T(8,128)(2,1)}, u32[]{:S(2)}) copy-start(bf16[4,1024,512]{2,1,0:T(8,128)(2,1)} %win_ref.1) | copy-start | bytes 12582916
  5.0 6.3 %collective-permute-start.3 = (bf16[32,1152]{1,0:T(8,128)(2,1)S(1)}, bf16[32,1152]{1,0:T(8,128)(2,1)S(1)}, u32[]{:S(2)}, u32[]{:S(2)}) collective-permute-start(bf16[32,1152]{1,0:T(8,128)(2,1)S(1)} %get-tuple-element.58), channel_id=1, source_target_pairs={{0,28},{1,29},{2,30},{3,31},{4,24},{5,25},{6,26},{7,27},{8,20},{9,... | collective-permute-start | bytes 221192 | tf_op jit(solution)/shard_map/ppermute | solution.py:208
  8.7 4.1 %collective-permute-start.2 = (bf16[32,1152]{1,0:T(8,128)(2,1)S(1)}, bf16[32,1152]{1,0:T(8,128)(2,1)S(1)}, u32[]{:S(2)}, u32[]{:S(2)}) collective-permute-start(bf16[32,1152]{1,0:T(8,128)(2,1)S(1)} %get-tuple-element.58), channel_id=1, source_target_pairs={{0,20},{1,21},{2,22},{3,23},{4,16},{5,17},{6,18},{7,19},{8,28},{9,... | collective-permute-start | bytes 221192 | tf_op jit(solution)/shard_map/ppermute | solution.py:208
  9.1 4.2 %collective-permute-start.1 = (bf16[32,1152]{1,0:T(8,128)(2,1)S(1)}, bf16[32,1152]{1,0:T(8,128)(2,1)S(1)}, u32[]{:S(2)}, u32[]{:S(2)}) collective-permute-start(bf16[32,1152]{1,0:T(8,128)(2,1)S(1)} %get-tuple-element.58), channel_id=1, source_target_pairs={{0,12},{1,13},{2,14},{3,15},{4,8},{5,9},{6,10},{7,11},{8,4},{9,5},... | collective-permute-start | bytes 221192 | tf_op jit(solution)/shard_map/ppermute | solution.py:208
  15.0 1.3 %collective-permute-start.4 = (bf16[32,512]{1,0:T(8,128)(2,1)S(1)}, bf16[32,512]{1,0:T(8,128)(2,1)S(1)}, u32[]{:S(2)}, u32[]{:S(2)}) collective-permute-start(bf16[32,512]{1,0:T(8,128)(2,1)S(1)} %get-tuple-element.70), channel_id=1, source_target_pairs={{0,4},{1,5},{2,6},{3,7},{4,0},{5,1},{6,2},{7,3},{8,12},{9,13},{10,... | collective-permute-start | bytes 98312 | tf_op jit(solution)/shard_map/ppermute | solution.py:208
  16.3 5.3 %collective-permute-start.7 = (bf16[32,512]{1,0:T(8,128)(2,1)S(1)}, bf16[32,512]{1,0:T(8,128)(2,1)S(1)}, u32[]{:S(2)}, u32[]{:S(2)}) collective-permute-start(bf16[32,512]{1,0:T(8,128)(2,1)S(1)} %get-tuple-element.79), channel_id=1, source_target_pairs={{0,24},{1,25},{2,26},{3,27},{4,28},{5,29},{6,30},{7,31},{8,16},{9,... | collective-permute-start | bytes 98312 | tf_op jit(solution)/shard_map/ppermute | solution.py:208
  17.9 4.0 %collective-permute-start.6 = (bf16[32,512]{1,0:T(8,128)(2,1)S(1)}, bf16[32,512]{1,0:T(8,128)(2,1)S(1)}, u32[]{:S(2)}, u32[]{:S(2)}) collective-permute-start(bf16[32,512]{1,0:T(8,128)(2,1)S(1)} %get-tuple-element.79), channel_id=1, source_target_pairs={{0,20},{1,21},{2,22},{3,23},{4,16},{5,17},{6,18},{7,19},{8,28},{9,... | collective-permute-start | bytes 98312 | tf_op jit(solution)/shard_map/ppermute | solution.py:208
  19.0 3.3 %collective-permute-start.5 = (bf16[32,512]{1,0:T(8,128)(2,1)S(1)}, bf16[32,512]{1,0:T(8,128)(2,1)S(1)}, u32[]{:S(2)}, u32[]{:S(2)}) collective-permute-start(bf16[32,512]{1,0:T(8,128)(2,1)S(1)} %get-tuple-element.79), channel_id=1, source_target_pairs={{0,12},{1,13},{2,14},{3,15},{4,8},{5,9},{6,10},{7,11},{8,4},{9,5},... | collective-permute-start | bytes 98312 | tf_op jit(solution)/shard_map/ppermute | solution.py:208
  23.0 9.7 %collective-permute-start.10 = (bf16[32,512]{1,0:T(8,128)(2,1)S(1)}, bf16[32,512]{1,0:T(8,128)(2,1)S(1)}, u32[]{:S(2)}, u32[]{:S(2)}) collective-permute-start(bf16[32,512]{1,0:T(8,128)(2,1)S(1)} %get-tuple-element.90), channel_id=1, source_target_pairs={{0,3},{1,2},{2,1},{3,0},{4,7},{5,6},{6,5},{7,4},{8,11},{9,10},{10,... | collective-permute-start | bytes 98312 | tf_op jit(solution)/shard_map/ppermute | solution.py:208
  26.6 6.1 %collective-permute-start.9 = (bf16[32,512]{1,0:T(8,128)(2,1)S(1)}, bf16[32,512]{1,0:T(8,128)(2,1)S(1)}, u32[]{:S(2)}, u32[]{:S(2)}) collective-permute-start(bf16[32,512]{1,0:T(8,128)(2,1)S(1)} %get-tuple-element.90), channel_id=1, source_target_pairs={{0,6},{1,7},{2,4},{3,5},{4,2},{5,3},{6,0},{7,1},{8,14},{9,15},{10,... | collective-permute-start | bytes 98312 | tf_op jit(solution)/shard_map/ppermute | solution.py:208
  26.6 6.1 %collective-permute-start.8 = (bf16[32,512]{1,0:T(8,128)(2,1)S(1)}, bf16[32,512]{1,0:T(8,128)(2,1)S(1)}, u32[]{:S(2)}, u32[]{:S(2)}) collective-permute-start(bf16[32,512]{1,0:T(8,128)(2,1)S(1)} %get-tuple-element.90), channel_id=1, source_target_pairs={{0,5},{1,4},{2,7},{3,6},{4,1},{5,0},{6,3},{7,2},{8,13},{9,12},{10,... | collective-permute-start | bytes 98312 | tf_op jit(solution)/shard_map/ppermute | solution.py:208
  27.8 11.7 %all-to-all-start = ((f32[4,40,256]{2,1,0:T(8,128)}), f32[4,40,256]{2,1,0:T(8,128)S(1)}, u32[]{:S(2)}, u32[]{:S(2)}) async-start(f32[4,40,256]{2,1,0:T(8,128)} %pack.1), calls=%async_computation | async-start | bytes 327680 | tf_op jit(solution)/shard_map/all_to_all | solution.py:295
  32.7 6.9 %collective-permute-start.11 = (bf16[128,512]{1,0:T(8,128)(2,1)S(1)}, bf16[128,512]{1,0:T(8,128)(2,1)S(1)}, u32[]{:S(2)}, u32[]{:S(2)}) collective-permute-start(bf16[128,512]{1,0:T(8,128)(2,1)S(1)} %constant_dynamic-update-slice_fusion.mine_ref), channel_id=1, source_target_pairs={{0,4},{1,5},{2,6},{3,7},{4,0},{5,1},{6,2},{7,3},{8,12},{9,13},{10,... | collective-permute-start | bytes 393224 | tf_op jit(solution)/shard_map/ppermute | solution.py:208
